TPU v7x, 32 devices: a whole 2x2x4 slice. The times are simulated.
32 devices in a mesh: cells: 16 (over z, x, core), ens: 2 (over y).
Axes of the slice: x: 2, y: 2, z: 4, core: 2. Of those that a mesh axis runs over, the one named last changes fastest.
Arguments:
- later_adjoint: float32 [4, 4, 32, 8, 128], P('ens', None, 'cells'), may hold values from -6 to 6
- coupling: bfloat16 [4, 6, 4, 4, 32, 8, 128], P('ens', None, None, None, 'cells'), may hold values from -0.59765625 to 0.59765625
- diag_inverse: bfloat16 [4, 4, 4, 32, 8, 128], P('ens', None, None, 'cells'), may hold values from -0.7 to 1.6, as said below
- sensitivity: bfloat16 [4, 4, 32, 8, 128, 128], P('ens', None, 'cells'), may hold values from -0.0625 to 0.0625
- well_cells: int32 [256], replicated, may hold values from 0 to 32767
- well_misfit: float32 [4, 4, 256], P('ens'), may hold values from -6 to 6
- block_map: int32 [32, 8, 128], P('cells'), may hold values from 0 to 63, as said below
Outputs:
- adjoint: float32 [4, 4, 32, 8, 128], P('ens', None, 'cells')
- gradient: float32 [64, 128], P('cells')
Inputs may be any that keep to these rules, and one draw needn't show every extreme that they name: `block_map`: of the cells of each slab of 2 planes along the first dimension (x from i * 2 to i * 2 + 1), exactly 128 map to blocks whose number divided by 4 (rounded down) equals any given j. `diag_inverse`: each block is the inverse of a diagonal block; its diagonal entries lie in 0.4 to 1.6. `well_cells`: wells may share a cell.
All inputs are finite; a program needn't handle non-finite values.
Results may differ from a plain program's by a relative error of at most 0.0003.
Values sent between devices are 32-bit elements; how exact they have to be, the bound alone decides.
A program may use at most 64 MiB of HBM per device.

v0:
```python
import jax
import jax.numpy as jnp
from jax import lax
from jax.sharding import PartitionSpec as P

ITERS = 4
BLK_DEV = 4


def from_behind(value, axis, by):
    devices = lax.axis_size(axis)
    pairs = [(i, i + by) for i in range(devices) if 0 <= i + by < devices]
    return lax.ppermute(value, axis, pairs)


def move_along(field, axis, forward):
    length = field.shape[axis]
    shape = list(field.shape)
    shape[axis] = 1
    zeros = jnp.zeros(shape, jnp.float32)
    if forward:
        return jnp.concatenate(
            [zeros, lax.slice_in_dim(field, 0, length - 1, axis=axis)], axis=axis
        )
    return jnp.concatenate([lax.slice_in_dim(field, 1, length, axis=axis), zeros], axis=axis)


def coupling_sum(adjoint, coupling):
    terms = jnp.sum(coupling.astype(jnp.float32) * adjoint[:, None, :, None], axis=2)
    upward = terms[:, 0]
    downward = terms[:, 1]
    planes = upward.shape[2]
    from_below = from_behind(upward[:, :, planes - 1 :], "cells", 1)
    from_above = from_behind(downward[:, :, :1], "cells", -1)
    total = jnp.concatenate([from_below, upward[:, :, : planes - 1]], axis=2)
    total = total + jnp.concatenate([downward[:, :, 1:], from_above], axis=2)
    total = total + move_along(terms[:, 2], 3, True) + move_along(terms[:, 3], 3, False)
    total = total + move_along(terms[:, 4], 4, True) + move_along(terms[:, 5], 4, False)
    return total


def apply_inverse(diag_inverse, source):
    return jnp.sum(diag_inverse.astype(jnp.float32) * source[:, :, None], axis=1)


def body(later_adjoint, coupling, diag_inverse, sensitivity, well_cells, well_misfit, block_map):
    members, unknowns, planes, columns, layers = later_adjoint.shape
    count = planes * columns * layers
    ranks = lax.axis_size("cells")
    first_cell = lax.axis_index("cells") * count
    cell_ids = first_cell + jnp.arange(count, dtype=jnp.int32)
    onehot = (well_cells[:, None] == cell_ids[None, :]).astype(jnp.float32)
    injected = jnp.dot(
        well_misfit.reshape(members * unknowns, -1),
        onehot,
        precision=lax.Precision.HIGHEST,
        preferred_element_type=jnp.float32,
    )
    source = later_adjoint + injected.reshape(later_adjoint.shape)
    adjoint = apply_inverse(diag_inverse, source)
    for sweep in range(ITERS):
        adjoint = apply_inverse(diag_inverse, source - coupling_sum(adjoint, coupling))
    params = sensitivity.shape[-1]
    adjoint_flat = adjoint.reshape(members, unknowns, count)
    sens_flat = sensitivity.reshape(members, unknowns, count, params)
    cell_grad = jnp.sum(adjoint_flat[..., None] * sens_flat.astype(jnp.float32), axis=(0, 1))
    flat_map = block_map.reshape(-1)
    owner = flat_map // BLK_DEV
    order = jnp.argsort(owner, stable=True)
    per_owner = count // ranks
    send_rows = cell_grad[order].reshape(ranks, per_owner, params)
    send_ids = (flat_map[order] % BLK_DEV).astype(jnp.float32).reshape(ranks, per_owner)
    got_rows, got_ids = (
        lax.all_to_all(send_rows, "cells", split_axis=0, concat_axis=0, tiled=True),
        lax.all_to_all(send_ids, "cells", split_axis=0, concat_axis=0, tiled=True),
    )
    owned = jax.ops.segment_sum(
        got_rows.reshape(-1, params), got_ids.reshape(-1).astype(jnp.int32), num_segments=BLK_DEV
    )
    gradient = lax.psum(owned, "ens")
    return (adjoint, gradient)


def solution(mesh):
    placed = (
        P("ens", None, "cells", None, None),
        P("ens", None, None, None, "cells", None, None),
        P("ens", None, None, "cells", None, None),
        P("ens", None, "cells", None, None, None),
        P(),
        P("ens", None, None),
        P("cells", None, None),
    )
    return jax.shard_map(
        body,
        mesh=mesh,
        in_specs=placed,
        out_specs=(P("ens", None, "cells", None, None), P("cells", None)),
        check_vma=False,
    )
```

profile of v0, /device:TPU:0, one launch (start us, length us, event | category | flops | bytes accessed | tf_op | source)
XLA Modules:
  0.0 115.3 jit_solution(3998718716475427112)
XLA Ops:
  0.7 0.8 reshape.110
  1.4 1.4 %fusion.6 = f32[1,8,16,128]{3,1,2,0:T(8,128)S(1)} fusion(f32[8,256]{1,0:T(8,128)S(1)} %reshape.110, s32[2048]{0:T(1024)S(1)} %iota_add_fusion, s32[256]{0:T(256)} %param.11), kind=kOutput, calls=%fused_computation.14 | convolution fusion | flops 50855936 | bytes 82944 | tf_op jit(solution)/shard_map/dot_general | solution.py:53
  2.9 0.9 add.130
  3.7 0.9 fusion.11
  4.7 0.2 fusion.2
  4.9 1.3 %collective-permute-start.1 = (f32[2,4,1,8,128]{4,3,2,1,0:T(8,128)S(1)}, f32[2,4,1,8,128]{4,3,2,1,0:T(8,128)S(1)}, u32[]{:S(2)}, u32[]{:S(2)}) collective-permute-start(f32[2,4,1,8,128]{4,3,2,1,0:T(8,128)S(1)} %get-tuple-element.41), channel_id=1, source_target_pairs={{2,0},{4,2},{6,4},{8,6},{10,8},{12,10},{14,12},{16,14},{18,16},{20... | collective-permute-start | bytes 98312 | tf_op jit(solution)/shard_map/ppermute | solution.py:13
  6.3 3.0 %collective-permute-start = (f32[2,4,1,8,128]{4,3,2,1,0:T(8,128)S(1)}, f32[2,4,1,8,128]{4,3,2,1,0:T(8,128)S(1)}, u32[]{:S(2)}, u32[]{:S(2)}) collective-permute-start(f32[2,4,1,8,128]{4,3,2,1,0:T(8,128)S(1)} %get-tuple-element.42), channel_id=1, source_target_pairs={{0,2},{2,4},{4,6},{6,8},{8,10},{10,12},{12,14},{14,16},{16,18},{18... | collective-permute-start | bytes 98312 | tf_op jit(solution)/shard_map/ppermute | solution.py:13
  9.4 0.7 collective-permute-done
  10.5 1.3 %collective-permute-start.3 = (f32[2,4,1,8,128]{4,3,2,1,0:T(8,128)S(1)}, f32[2,4,1,8,128]{4,3,2,1,0:T(8,128)S(1)}, u32[]{:S(2)}, u32[]{:S(2)}) collective-permute-start(f32[2,4,1,8,128]{4,3,2,1,0:T(8,128)S(1)} %get-tuple-element.37), channel_id=1, source_target_pairs={{2,0},{4,2},{6,4},{8,6},{10,8},{12,10},{14,12},{16,14},{18,16},{20... | collective-permute-start | bytes 98312 | tf_op jit(solution)/shard_map/ppermute | solution.py:13
  11.8 5.3 %collective-permute-start.2 = (f32[2,4,1,8,128]{4,3,2,1,0:T(8,128)S(1)}, f32[2,4,1,8,128]{4,3,2,1,0:T(8,128)S(1)}, u32[]{:S(2)}, u32[]{:S(2)}) collective-permute-start(f32[2,4,1,8,128]{4,3,2,1,0:T(8,128)S(1)} %get-tuple-element.38), channel_id=1, source_target_pairs={{0,2},{2,4},{4,6},{6,8},{8,10},{10,12},{12,14},{14,16},{16,18},{18... | collective-permute-start | bytes 98312 | tf_op jit(solution)/shard_map/ppermute | solution.py:13
  17.1 5.0 %sort.17 = (s32[2048]{0:T(1024)}, s32[2048]{0:T(1024)S(1)}) sort(s32[2048]{0:T(1024)S(1)} %add_select_fusion, s32[2048]{0:T(1024)S(1)} %iota.10), dimensions={0}, to_apply=%region_9.0 | sort | flops 22528 | bytes 32768 | tf_op jit(solution)/shard_map/jit(argsort)/sort | solution.py:69
  22.6 1.3 %collective-permute-start.5 = (f32[2,4,1,8,128]{4,3,2,1,0:T(8,128)S(1)}, f32[2,4,1,8,128]{4,3,2,1,0:T(8,128)S(1)}, u32[]{:S(2)}, u32[]{:S(2)}) collective-permute-start(f32[2,4,1,8,128]{4,3,2,1,0:T(8,128)S(1)} %get-tuple-element.33), channel_id=1, source_target_pairs={{2,0},{4,2},{6,4},{8,6},{10,8},{12,10},{14,12},{16,14},{18,16},{20... | collective-permute-start | bytes 98312 | tf_op jit(solution)/shard_map/ppermute | solution.py:13
  24.0 4.9 %collective-permute-start.4 = (f32[2,4,1,8,128]{4,3,2,1,0:T(8,128)S(1)}, f32[2,4,1,8,128]{4,3,2,1,0:T(8,128)S(1)}, u32[]{:S(2)}, u32[]{:S(2)}) collective-permute-start(f32[2,4,1,8,128]{4,3,2,1,0:T(8,128)S(1)} %get-tuple-element.34), channel_id=1, source_target_pairs={{0,2},{2,4},{4,6},{6,8},{8,10},{10,12},{12,14},{14,16},{16,18},{18... | collective-permute-start | bytes 98312 | tf_op jit(solution)/shard_map/ppermute | solution.py:13
  28.8 11.8 %gather_fusion = s32[2048]{0:T(1024)S(1)} fusion(s32[2048]{0:T(1024)S(1)} %bitcast.115, s32[2048]{0:T(1024)S(1)} %fusion.37), kind=kCustom, calls=%fused_computation | custom fusion | bytes 24576 | tf_op jit(solution)/shard_map/gather | solution.py:72
  41.1 1.3 %collective-permute-start.7 = (f32[2,4,1,8,128]{4,3,2,1,0:T(8,128)S(1)}, f32[2,4,1,8,128]{4,3,2,1,0:T(8,128)S(1)}, u32[]{:S(2)}, u32[]{:S(2)}) collective-permute-start(f32[2,4,1,8,128]{4,3,2,1,0:T(8,128)S(1)} %get-tuple-element.29), channel_id=1, source_target_pairs={{2,0},{4,2},{6,4},{8,6},{10,8},{12,10},{14,12},{16,14},{18,16},{20... | collective-permute-start | bytes 98312 | tf_op jit(solution)/shard_map/ppermute | solution.py:13
  42.4 4.3 %collective-permute-start.6 = (f32[2,4,1,8,128]{4,3,2,1,0:T(8,128)S(1)}, f32[2,4,1,8,128]{4,3,2,1,0:T(8,128)S(1)}, u32[]{:S(2)}, u32[]{:S(2)}) collective-permute-start(f32[2,4,1,8,128]{4,3,2,1,0:T(8,128)S(1)} %get-tuple-element.30), channel_id=1, source_target_pairs={{0,2},{2,4},{4,6},{6,8},{8,10},{10,12},{12,14},{14,16},{16,18},{18... | collective-permute-start | bytes 98312 | tf_op jit(solution)/shard_map/ppermute | solution.py:13
  46.7 0.6 fusion.38
  47.3 9.8 %all-to-all-start = ((f32[16,1,128]{2,1,0:T(1,128)}), f32[16,1,128]{2,1,0:T(1,128)S(1)}, u32[]{:S(2)}, u32[]{:S(2)}) async-start(f32[16,1,128]{2,1,0:T(1,128)} %fusion.38), calls=%async_computation | async-start | bytes 16384 | tf_op jit(solution)/shard_map/all_to_all | solution.py:75
  57.4 4.5 %multiply_reduce_fusion = f32[2,8,128,128]{3,2,1,0:T(8,128)S(1)} fusion(bf16[2,4,2,8,128,128]{5,4,3,2,1,0:T(8,128)(2,1)} %param.10, f32[2,4,2,8,128]{4,3,2,1,0:T(8,128)S(1)} %fusion.15), kind=kLoop, calls=%fused_computation.3 | loop fusion | flops 6029312 | bytes 5308416 | tf_op jit(solution)/shard_map/reduce_sum | solution.py:66
  61.9 7.6 %gather_fusion.1 = f32[2048,128]{1,0:T(8,128)} fusion(f32[2048,128]{1,0:T(8,128)S(1)} %bitcast.116, s32[2048]{0:T(1024)S(1)} %fusion.37), kind=kCustom, calls=%fused_computation.1 | custom fusion | bytes 2105344 | tf_op jit(solution)/shard_map/gather | solution.py:71
  69.4 6.0 %all-to-all-start.1 = ((f32[16,128,128]{2,1,0:T(8,128)}), f32[16,128,128]{2,1,0:T(8,128)S(1)}, u32[]{:S(2)}, u32[]{:S(2)}) async-start(f32[16,128,128]{2,1,0:T(8,128)} %bitcast.29), calls=%async_computation.1 | async-start | bytes 2097152 | tf_op jit(solution)/shard_map/all_to_all | solution.py:74
  75.5 22.9 %all-to-all-done.1 = f32[16,128,128]{2,1,0:T(8,128)S(1)} async-done(((f32[16,128,128]{2,1,0:T(8,128)}), f32[16,128,128]{2,1,0:T(8,128)S(1)}, u32[]{:S(2)}, u32[]{:S(2)}) %all-to-all-start.1) | async-done | bytes 1048608 | tf_op jit(solution)/shard_map/all_to_all | solution.py:74
  98.3 11.4 %scatter_custom_fusion = f32[4,128]{1,0:T(4,128)S(1)} fusion(s32[2048]{0:T(1024)S(1)} %bitcast.128, f32[2048,128]{1,0:T(8,128)S(1)} %bitcast.117, f32[]{:T(128)} %constant.36.clone.1), kind=kCustom, calls=%fused_computation.90 | custom fusion | flops 262144 | bytes 2052 | tf_op jit(solution)/shard_map/scatter-add | solution.py:77
  109.8 5.5 %psum.7 = f32[4,128]{1,0:T(4,128)} all-reduce(f32[4,128]{1,0:T(4,128)S(1)} %scatter_custom_fusion), channel_id=1, replica_groups=mesh['cells'=16,'ens'=2] {'ens'}, use_global_device_ids=true, to_apply=%region_12.13 | all-reduce | flops 512 | bytes 4096 | tf_op jit(solution)/shard_map/psum | solution.py:80
  (53 shorter events, 1.6 us)
Async XLA Ops:
  0.6 4.1 %copy-start.1 = (bf16[2,6,4,4,2,8,128]{6,5,4,3,2,1,0:T(8,128)(2,1)S(1)}, bf16[2,6,4,4,2,8,128]{6,5,4,3,2,1,0:T(8,128)(2,1)}, u32[]{:S(2)}) copy-start(bf16[2,6,4,4,2,8,128]{6,5,4,3,2,1,0:T(8,128)(2,1)} %param.8) | copy-start | bytes 2359300
  4.7 5.5 %copy-start.2 = (bf16[2,4,4,2,8,128]{5,4,3,2,1,0:T(8,128)(2,1)S(1)}, bf16[2,4,4,2,8,128]{5,4,3,2,1,0:T(8,128)(2,1)}, u32[]{:S(2)}) copy-start(bf16[2,4,4,2,8,128]{5,4,3,2,1,0:T(8,128)(2,1)} %param.9) | copy-start | bytes 393220
  4.9 4.5 %collective-permute-start.1 = (f32[2,4,1,8,128]{4,3,2,1,0:T(8,128)S(1)}, f32[2,4,1,8,128]{4,3,2,1,0:T(8,128)S(1)}, u32[]{:S(2)}, u32[]{:S(2)}) collective-permute-start(f32[2,4,1,8,128]{4,3,2,1,0:T(8,128)S(1)} %get-tuple-element.41), channel_id=1, source_target_pairs={{2,0},{4,2},{6,4},{8,6},{10,8},{12,10},{14,12},{16,14},{18,16},{20... | collective-permute-start | bytes 98312 | tf_op jit(solution)/shard_map/ppermute | solution.py:13
  6.3 3.9 %collective-permute-start = (f32[2,4,1,8,128]{4,3,2,1,0:T(8,128)S(1)}, f32[2,4,1,8,128]{4,3,2,1,0:T(8,128)S(1)}, u32[]{:S(2)}, u32[]{:S(2)}) collective-permute-start(f32[2,4,1,8,128]{4,3,2,1,0:T(8,128)S(1)} %get-tuple-element.42), channel_id=1, source_target_pairs={{0,2},{2,4},{4,6},{6,8},{8,10},{10,12},{12,14},{14,16},{16,18},{18... | collective-permute-start | bytes 98312 | tf_op jit(solution)/shard_map/ppermute | solution.py:13
  9.4 7.7 %copy-start = (s32[2,8,128]{2,1,0:T(8,128)S(1)}, s32[2,8,128]{2,1,0:T(8,128)}, u32[]{:S(2)}) copy-start(s32[2,8,128]{2,1,0:T(8,128)} %param.13) | copy-start | bytes 24580
  10.5 11.8 %collective-permute-start.3 = (f32[2,4,1,8,128]{4,3,2,1,0:T(8,128)S(1)}, f32[2,4,1,8,128]{4,3,2,1,0:T(8,128)S(1)}, u32[]{:S(2)}, u32[]{:S(2)}) collective-permute-start(f32[2,4,1,8,128]{4,3,2,1,0:T(8,128)S(1)} %get-tuple-element.37), channel_id=1, source_target_pairs={{2,0},{4,2},{6,4},{8,6},{10,8},{12,10},{14,12},{16,14},{18,16},{20... | collective-permute-start | bytes 98312 | tf_op jit(solution)/shard_map/ppermute | solution.py:13
  11.8 10.5 %collective-permute-start.2 = (f32[2,4,1,8,128]{4,3,2,1,0:T(8,128)S(1)}, f32[2,4,1,8,128]{4,3,2,1,0:T(8,128)S(1)}, u32[]{:S(2)}, u32[]{:S(2)}) collective-permute-start(f32[2,4,1,8,128]{4,3,2,1,0:T(8,128)S(1)} %get-tuple-element.38), channel_id=1, source_target_pairs={{0,2},{2,4},{4,6},{6,8},{8,10},{10,12},{12,14},{14,16},{16,18},{18... | collective-permute-start | bytes 98312 | tf_op jit(solution)/shard_map/ppermute | solution.py:13
  22.6 18.1 %collective-permute-start.5 = (f32[2,4,1,8,128]{4,3,2,1,0:T(8,128)S(1)}, f32[2,4,1,8,128]{4,3,2,1,0:T(8,128)S(1)}, u32[]{:S(2)}, u32[]{:S(2)}) collective-permute-start(f32[2,4,1,8,128]{4,3,2,1,0:T(8,128)S(1)} %get-tuple-element.33), channel_id=1, source_target_pairs={{2,0},{4,2},{6,4},{8,6},{10,8},{12,10},{14,12},{16,14},{18,16},{20... | collective-permute-start | bytes 98312 | tf_op jit(solution)/shard_map/ppermute | solution.py:13
  24.0 16.8 %collective-permute-start.4 = (f32[2,4,1,8,128]{4,3,2,1,0:T(8,128)S(1)}, f32[2,4,1,8,128]{4,3,2,1,0:T(8,128)S(1)}, u32[]{:S(2)}, u32[]{:S(2)}) collective-permute-start(f32[2,4,1,8,128]{4,3,2,1,0:T(8,128)S(1)} %get-tuple-element.34), channel_id=1, source_target_pairs={{0,2},{2,4},{4,6},{6,8},{8,10},{10,12},{12,14},{14,16},{16,18},{18... | collective-permute-start | bytes 98312 | tf_op jit(solution)/shard_map/ppermute | solution.py:13
  41.1 16.1 %collective-permute-start.7 = (f32[2,4,1,8,128]{4,3,2,1,0:T(8,128)S(1)}, f32[2,4,1,8,128]{4,3,2,1,0:T(8,128)S(1)}, u32[]{:S(2)}, u32[]{:S(2)}) collective-permute-start(f32[2,4,1,8,128]{4,3,2,1,0:T(8,128)S(1)} %get-tuple-element.29), channel_id=1, source_target_pairs={{2,0},{4,2},{6,4},{8,6},{10,8},{12,10},{14,12},{16,14},{18,16},{20... | collective-permute-start | bytes 98312 | tf_op jit(solution)/shard_map/ppermute | solution.py:13
  42.4 14.8 %collective-permute-start.6 = (f32[2,4,1,8,128]{4,3,2,1,0:T(8,128)S(1)}, f32[2,4,1,8,128]{4,3,2,1,0:T(8,128)S(1)}, u32[]{:S(2)}, u32[]{:S(2)}) collective-permute-start(f32[2,4,1,8,128]{4,3,2,1,0:T(8,128)S(1)} %get-tuple-element.30), channel_id=1, source_target_pairs={{0,2},{2,4},{4,6},{6,8},{8,10},{10,12},{12,14},{14,16},{16,18},{18... | collective-permute-start | bytes 98312 | tf_op jit(solution)/shard_map/ppermute | solution.py:13
  47.3 22.1 %all-to-all-start = ((f32[16,1,128]{2,1,0:T(1,128)}), f32[16,1,128]{2,1,0:T(1,128)S(1)}, u32[]{:S(2)}, u32[]{:S(2)}) async-start(f32[16,1,128]{2,1,0:T(1,128)} %fusion.38), calls=%async_computation | async-start | bytes 16384 | tf_op jit(solution)/shard_map/all_to_all | solution.py:75
  57.4 4.5 %copy-start.3 = (f32[2,4,2,8,128]{4,3,2,1,0:T(8,128)}, f32[2,4,2,8,128]{4,3,2,1,0:T(8,128)S(1)}, u32[]{:S(2)}) copy-start(f32[2,4,2,8,128]{4,3,2,1,0:T(8,128)S(1)} %fusion.15) | copy-start | bytes 196612
  69.4 28.9 %all-to-all-start.1 = ((f32[16,128,128]{2,1,0:T(8,128)}), f32[16,128,128]{2,1,0:T(8,128)S(1)}, u32[]{:S(2)}, u32[]{:S(2)}) async-start(f32[16,128,128]{2,1,0:T(8,128)} %bitcast.29), calls=%async_computation.1 | async-start | bytes 2097152 | tf_op jit(solution)/shard_map/all_to_all | solution.py:74
where the time goes:
time: 117 us; the launch traced here: 115 us
  starting transfers between devices  38.4 us (33%)
  other arithmetic  24.6 us (21%)
  waiting for transfers between devices  23.6 us (20%)
  local copies, waits for them, and re-layouts  20.7 us (18%)
  blocking collectives  5.5 us (5%)
  matrix products  1.43 us (1%)
    all_to_all x1, waiting for transfers between devices, body(): lax.all_to_all(send_rows, 'cells', split_axis=0, concat_axis=0, tiled=True)  22.9 us
    ppermute x8, starting transfers between devices, from_behind(): return lax.ppermute(value, axis, pairs)  22.6 us
    gather x1, local copies, waits for them, and re-layouts, body(): flat_map[order] % BLK_DEV  11.8 us
    scatter-add x1, other arithmetic, body(): jax.ops.segment_sum(got_rows.reshape(-1, params), got_ids.reshape(-1).ast...  11.4 us
    all_to_all x1, starting transfers between devices, body(): lax.all_to_all(send_ids, 'cells', split_axis=0, concat_axis=0, tiled=True)  9.8 us
    gather x1, local copies, waits for them, and re-layouts, body(): send_rows = cell_grad[order].reshape(ranks, per_owner, params)  7.58 us
    all_to_all x1, starting transfers between devices, body(): lax.all_to_all(send_rows, 'cells', split_axis=0, concat_axis=0, tiled=True)  6.01 us
    psum x1, blocking collectives, body(): gradient = lax.psum(owned, 'ens')  5.5 us
  transfers between devices with their start and end apart: 10, of which 2 were waited for; matrix products, arithmetic and copies ran while one was open for 26% of the time, Pallas kernels for 0%

commit v1 on v0

v1 whole, which is shorter than its diff:
```python
import functools

import jax
import jax.numpy as jnp
from jax import lax
from jax.experimental import pallas as pl
from jax.experimental.pallas import tpu as pltpu
from jax.sharding import PartitionSpec as P

ITERS = 4
MESH = pl.DeviceIdType.MESH
F32 = jnp.float32
BF16 = jnp.bfloat16


def for_each(count, step):
    if count <= 64:
        for i in range(count):
            step(i)
    else:
        def body(i, carry):
            step(i)
            return carry

        lax.fori_loop(0, count, body, 0)


def split(value):
    high = value.astype(BF16).astype(F32)
    return high, value - high


def kernel(
    ranks, groups, blocks,
    later_hbm, coup_hbm, diag_hbm, sens_hbm, wells_hbm, misfit_hbm, map_hbm,
    adj_hbm, grad_ref,
    later, coup, diag, sens, wells, misfit, bmap, adj, source,
    up_send, down_send, below, above, mask, lhs, part, got,
    load_sem, sens_sem, adj_sem, up_ssem, up_rsem, down_ssem, down_rsem, part_ssem, part_rsem,
):
    members, unknowns, planes, columns, layers = later.shape
    rows = planes * columns
    count = rows * layers
    devices = ranks * groups
    blk_dev = blocks // ranks
    me_c = lax.axis_index("cells")
    me_e = lax.axis_index("ens")
    me = me_c * groups + me_e

    def other(step):
        at = me + step + 1
        at = jnp.where(at >= devices, at - devices, at)
        return at // groups, at % groups

    barrier = pltpu.get_barrier_semaphore()

    def greet(step):
        c, e = other(step)
        pl.semaphore_signal(barrier, inc=1, device_id=(c, e), device_id_type=MESH)

    loads = [
        pltpu.make_async_copy(src, dst, load_sem.at[i])
        for i, (src, dst) in enumerate(
            [
                (wells_hbm, wells), (misfit_hbm, misfit), (later_hbm, later), (diag_hbm, diag),
                (coup_hbm, coup), (map_hbm, bmap),
            ]
        )
    ]
    for load in loads:
        load.start()
    fields = members * unknowns
    sens_loads = [
        pltpu.make_async_copy(sens_hbm.at[i], sens.at[i], sens_sem.at[i]) for i in range(fields)
    ]
    for load in sens_loads:
        load.start()
    for_each(devices - 1, greet)

    loads[0].wait()
    loads[1].wait()
    total_wells = wells.shape[1]
    rel = wells[...] - me_c * count
    row_lo = lax.broadcasted_iota(jnp.int32, (rows, total_wells), 0) * layers
    in_row = (rel >= row_lo) & (rel < row_lo + layers)
    lane = wells[...] & (layers - 1)
    at_lane = lax.broadcasted_iota(jnp.int32, (layers, total_wells), 0) == lane
    at_lane = jnp.where(at_lane, 1.0, 0.0).astype(BF16)
    parts = [[], [], []]
    for m in range(members):
        for u in range(unknowns):
            rest = jnp.broadcast_to(misfit[m, u : u + 1, :], (rows, total_wells))
            rest = jnp.where(in_row, rest, 0.0)
            for i in range(3):
                high, rest = split(rest)
                parts[i].append(high.astype(BF16))
    injected = jnp.zeros((fields * rows, layers), F32)
    for piece in parts:
        injected = injected + lax.dot_general(
            jnp.concatenate(piece, axis=0), at_lane, (((1,), (1,)), ((), ())),
            preferred_element_type=F32,
        )
    loads[2].wait()
    source[...] = later[...] + injected.reshape(later.shape)

    def inverse(m, rhs):
        out = None
        for w in range(unknowns):
            term = diag[m, w].astype(F32) * rhs[w][None]
            out = term if out is None else out + term
        return out

    loads[3].wait()
    now = [inverse(m, source[m]) for m in range(members)]
    loads[4].wait()
    loads[5].wait()
    pl.semaphore_wait(barrier, devices - 1)

    first = me_c == 0
    last = me_c == ranks - 1
    next_id = (jnp.minimum(me_c + 1, ranks - 1), me_e)
    prev_id = (jnp.maximum(me_c - 1, 0), me_e)

    def up_copy(k, m):
        return pltpu.make_async_remote_copy(
            src_ref=up_send.at[k, m], dst_ref=below.at[k, m], send_sem=up_ssem.at[k, m],
            recv_sem=up_rsem.at[k, m], device_id=next_id, device_id_type=MESH,
        )

    def down_copy(k, m):
        return pltpu.make_async_remote_copy(
            src_ref=down_send.at[k, m], dst_ref=above.at[k, m], send_sem=down_ssem.at[k, m],
            recv_sem=down_rsem.at[k, m], device_id=prev_id, device_id_type=MESH,
        )

    @pl.when(first)
    def _():
        below[...] = jnp.zeros_like(below)

    @pl.when(last)
    def _():
        above[...] = jnp.zeros_like(above)

    lane_at = lax.broadcasted_iota(jnp.int32, (unknowns, planes, columns, layers), 3)
    col_at = lax.broadcasted_iota(jnp.int32, (unknowns, planes, columns, layers), 2)

    def product(m, k, value, lo, hi):
        out = None
        for u in range(unknowns):
            term = coup[m, k, u, :, lo:hi].astype(F32) * value[u, lo:hi][None]
            out = term if out is None else out + term
        return out

    for k in range(ITERS):
        for m in range(members):
            up_send[k, m] = product(m, 0, now[m], planes - 1, planes)[:, 0]
            down_send[k, m] = product(m, 1, now[m], 0, 1)[:, 0]

            @pl.when(jnp.logical_not(last))
            def _(m=m):
                up_copy(k, m).start()

            @pl.when(jnp.logical_not(first))
            def _(m=m):
                down_copy(k, m).start()

        inner = []
        for m in range(members):
            up = product(m, 0, now[m], 0, planes - 1)
            down = product(m, 1, now[m], 1, planes)
            left = pltpu.roll(product(m, 2, now[m], 0, planes), 1, 2)
            total = jnp.where(col_at == 0, 0.0, left)
            left = pltpu.roll(product(m, 3, now[m], 0, planes), columns - 1, 2)
            total = total + jnp.where(col_at == columns - 1, 0.0, left)
            left = pltpu.roll(product(m, 4, now[m], 0, planes), 1, 3)
            total = total + jnp.where(lane_at == 0, 0.0, left)
            left = pltpu.roll(product(m, 5, now[m], 0, planes), layers - 1, 3)
            total = total + jnp.where(lane_at == layers - 1, 0.0, left)
            inner.append((source[m] - total, up, down))
        if k == 0:
            ids = lax.broadcasted_iota(jnp.int32, (blocks, layers), 0)
            for x in range(planes):
                for y in range(columns):
                    row = x * columns + y
                    hit = jnp.where(bmap[x, y : y + 1, :] == ids, 1.0, 0.0)
                    mask[:, row * layers : (row + 1) * layers] = hit.astype(BF16)
        after = []
        for m in range(members):
            rest, up, down = inner[m]

            @pl.when(jnp.logical_not(first))
            def _(m=m):
                up_copy(k, m).wait_recv()

            @pl.when(jnp.logical_not(last))
            def _(m=m):
                down_copy(k, m).wait_recv()

            rest = rest - jnp.concatenate([below[k, m][:, None], up], axis=1)
            rest = rest - jnp.concatenate([down, above[k, m][:, None]], axis=1)
            after.append(inverse(m, rest))
        now = after

    for m in range(members):
        adj[m] = now[m]
    save = pltpu.make_async_copy(adj, adj_hbm, adj_sem)
    save.start()

    def gather(i, total):
        pltpu.make_async_copy(sens_hbm.at[i], sens.at[i], sens_sem.at[i]).wait()
        high, low = split(adj[i // unknowns, i % unknowns])
        slot = i % 2
        for x in range(planes):
            for y in range(columns):
                row = x * columns + y
                cols = slice(row * layers, (row + 1) * layers)
                hot = mask[:, cols]
                for j, value in enumerate((high, low)):
                    wide = jnp.broadcast_to(value[x, y : y + 1], (16, layers)).astype(BF16)
                    wide = jnp.concatenate([wide] * (blocks // 16), axis=0)
                    lhs[slot, j * blocks : (j + 1) * blocks, cols] = hot * wide
        return total + jnp.dot(
            lhs[slot], sens[i].reshape(count, sens.shape[-1]), preferred_element_type=F32
        )

    total = jnp.zeros((2 * blocks, sens.shape[-1]), F32)
    total = lax.fori_loop(0, fields, gather, total, unroll=blocks <= 64)
    total = total[:blocks] + total[blocks:]
    for c in range(ranks):
        part[c] = total[c * blk_dev : (c + 1) * blk_dev]

    def part_copy(step):
        c, e = other(step)
        return pltpu.make_async_remote_copy(
            src_ref=part.at[c], dst_ref=got.at[step], send_sem=part_ssem, recv_sem=part_rsem,
            device_id=(c, e), device_id_type=MESH,
        )

    for_each(devices - 1, lambda step: part_copy(step).start())
    everything = pltpu.make_async_remote_copy(
        src_ref=got, dst_ref=got, send_sem=part_ssem, recv_sem=part_rsem,
        device_id=next_id, device_id_type=MESH,
    )
    everything.wait_recv()
    grad_ref[...] = part[me_c] + jnp.sum(got[...], axis=0)

    everything.wait_send()
    for k in range(ITERS):
        for m in range(members):
            @pl.when(jnp.logical_not(last))
            def _(k=k, m=m):
                up_copy(k, m).wait_send()

            @pl.when(jnp.logical_not(first))
            def _(k=k, m=m):
                down_copy(k, m).wait_send()

    save.wait()


def solution(mesh):
    ranks, groups = mesh.shape["cells"], mesh.shape["ens"]

    def body(later_adjoint, coupling, diag_inverse, sensitivity, well_cells, well_misfit, block_map):
        members, unknowns, planes, columns, layers = later_adjoint.shape
        params = sensitivity.shape[-1]
        rows = planes * columns
        blk_dev = 4
        blocks = ranks * blk_dev
        fields = members * unknowns
        sens = sensitivity.reshape(fields, rows, layers, params)
        wells = well_cells.reshape(1, -1)
        halo = (ITERS, members, unknowns, columns, layers)
        any_spec = pl.BlockSpec(memory_space=pl.ANY)
        dma = pltpu.SemaphoreType.DMA
        return pl.pallas_call(
            functools.partial(kernel, ranks, groups, blocks),
            out_shape=(
                jax.ShapeDtypeStruct(later_adjoint.shape, F32),
                jax.ShapeDtypeStruct((blk_dev, params), F32),
            ),
            in_specs=[any_spec] * 7,
            out_specs=(any_spec, pl.BlockSpec(memory_space=pltpu.VMEM)),
            scratch_shapes=[
                pltpu.VMEM(later_adjoint.shape, F32),
                pltpu.VMEM(coupling.shape, BF16),
                pltpu.VMEM(diag_inverse.shape, BF16),
                pltpu.VMEM(sens.shape, BF16),
                pltpu.VMEM(wells.shape, jnp.int32),
                pltpu.VMEM(well_misfit.shape, F32),
                pltpu.VMEM(block_map.shape, jnp.int32),
                pltpu.VMEM(later_adjoint.shape, F32),
                pltpu.VMEM(later_adjoint.shape, F32),
                pltpu.VMEM(halo, F32),
                pltpu.VMEM(halo, F32),
                pltpu.VMEM(halo, F32),
                pltpu.VMEM(halo, F32),
                pltpu.VMEM((blocks, rows * layers), BF16),
                pltpu.VMEM((2, 2 * blocks, rows * layers), BF16),
                pltpu.VMEM((ranks, blk_dev, params), F32),
                pltpu.VMEM((ranks * groups - 1, blk_dev, params), F32),
                dma((6,)),
                dma((fields,)),
                dma,
                dma((ITERS, members)),
                dma((ITERS, members)),
                dma((ITERS, members)),
                dma((ITERS, members)),
                dma,
                dma,
            ],
            compiler_params=pltpu.CompilerParams(collective_id=0, has_side_effects=True),
        )(later_adjoint, coupling, diag_inverse, sens, wells, well_misfit, block_map)

    placed = (
        P("ens", None, "cells", None, None),
        P("ens", None, None, None, "cells", None, None),
        P("ens", None, None, "cells", None, None),
        P("ens", None, "cells", None, None, None),
        P(),
        P("ens", None, None),
        P("cells", None, None),
    )
    return jax.shard_map(
        body,
        mesh=mesh,
        in_specs=placed,
        out_specs=(P("ens", None, "cells", None, None), P("cells", None)),
        check_vma=False,
    )
```

time: 117 us -> 28.8 us (0.25); the launches traced: 115 us -> 28.6 us
  starting transfers between devices: 38.4 us -> 0 us
  Pallas kernels: 0 us -> 25.2 us
  other arithmetic: 24.6 us -> 0 us
  waiting for transfers between devices: 23.6 us -> 0 us
  local copies, waits for them, and re-layouts: 20.7 us -> 2.72 us
  blocking collectives: 5.5 us -> 0 us
  matrix products: 1.43 us -> 0 us
    pallas_call x0 -> x1, Pallas kernels: none -> 25.2 us  [body(): pl.pallas_call(functools.partial(kernel, ranks, groups, blocks), out_shap...]
    all_to_all x2 -> x0, waiting for transfers between devices: 22.9 us -> none  [the longest x1 22.9 us: body(): lax.all_to_all(send_rows, 'cells', split_axis=0, concat_axis=0, tiled=True)]
    ppermute x8 -> x0, starting transfers between devices: 22.6 us -> none  [from_behind(): return lax.ppermute(value, axis, pairs)]
    gather x2 -> x0, local copies, waits for them, and re-layouts: 19.4 us -> none  [the longest x1 11.8 us: body(): flat_map[order] % BLK_DEV]
    all_to_all x2 -> x0, starting transfers between devices: 15.8 us -> none  [the longest x1 9.8 us: body(): lax.all_to_all(send_ids, 'cells', split_axis=0, concat_axis=0, tiled=True)]
    scatter-add x1 -> x0, other arithmetic: 11.4 us -> none  [body(): jax.ops.segment_sum(got_rows.reshape(-1, params), got_ids.reshape(-1).ast...]
    reduce_sum x10 -> x0, other arithmetic: 6.21 us -> none  [the longest x1 4.47 us: body(): jnp.sum(adjoint_flat[..., None] * sens_flat.astype(jnp.float32), axis=(0,...]
    psum x1 -> x0, blocking collectives: 5.5 us -> none  [body(): gradient = lax.psum(owned, 'ens')]
  transfers between devices with their start and end apart: 10 -> 0, of which waited for: 2 -> 0; matrix products, arithmetic and copies ran while one was open for 26% -> 0% of each run, Pallas kernels for 0% -> 0%
where the time goes in v1:
time: 28.8 us; the launch traced here: 28.6 us
  Pallas kernels  25.2 us (88%)
  local copies, waits for them, and re-layouts  2.72 us (9%)
  between operations  0.64 us (2%)
    pallas_call x1, Pallas kernels, body(): pl.pallas_call(functools.partial(kernel, ranks, groups, blocks), out_shap...  25.2 us
    unnamed x2, local copies, waits for them, and re-layouts  2.72 us

profile of v1, /device:TPU:0, one launch (start us, length us, event | category | flops | bytes accessed | tf_op | source)
XLA Modules:
  0.0 28.6 jit_solution(6863910971972395827)
XLA Ops:
  0.6 25.2 %shard_map.86 = (f32[2,4,2,8,128]{4,3,2,1,0:T(8,128)}, f32[4,128]{1,0:T(4,128)}) custom-call(f32[2,4,2,8,128]{4,3,2,1,0:T(8,128)} %later_hbm.1, bf16[2,6,4,4,2,8,128]{6,5,4,3,2,1,0:T(8,128)(2,1)} %coup_hbm.1, bf16[2,4,4,2,8,128]{5,4,3,2,1,0:T(8,128)(2,1)} %diag_hbm.1, bf16[8,16,128,128]{3,2,1,0:T(8,128)(2,1)} %bitcast.2, s32[1,256]{1,0:T(1,128)} %bitcast.3, ...), custom_call_target="tpu_custom_call" | custom-call | tf_op jit(solution)/shard_map/pallas_call | solution.py:276
  25.9 1.5 %copy.11 = f32[2,4,2,8,128]{4,3,2,1,0:T(8,128)} copy(f32[2,4,2,8,128]{4,3,2,1,0:T(8,128)} %get-tuple-element.4) | data formatting | bytes 131072
  27.3 1.2 %copy.12 = f32[4,128]{1,0:T(4,128)} copy(f32[4,128]{1,0:T(4,128)} %get-tuple-element.5) | data formatting | bytes 4096

commit v2 on v1

--- a/solution.py
+++ b/solution.py
@@ -33,10 +33,10 @@
 def kernel(
     ranks, groups, blocks,
     later_hbm, coup_hbm, diag_hbm, sens_hbm, wells_hbm, misfit_hbm, map_hbm,
-    adj_hbm, grad_ref,
-    later, coup, diag, sens, wells, misfit, bmap, adj, source,
+    adj, got_out,
+    later, coup, diag, sens, wells, misfit, bmap, source,
     up_send, down_send, below, above, mask, lhs, part, got,
-    load_sem, sens_sem, adj_sem, up_ssem, up_rsem, down_ssem, down_rsem, part_ssem, part_rsem,
+    load_sem, sens_sem, up_ssem, up_rsem, down_ssem, down_rsem, part_ssem, part_rsem,
 ):
     members, unknowns, planes, columns, layers = later.shape
     rows = planes * columns
@@ -113,8 +113,6 @@
     loads[3].wait()
     now = [inverse(m, source[m]) for m in range(members)]
     loads[4].wait()
-    loads[5].wait()
-    pl.semaphore_wait(barrier, devices - 1)
 
     first = me_c == 0
     last = me_c == ranks - 1
@@ -151,39 +149,46 @@
             out = term if out is None else out + term
         return out
 
+    def edges(k, m, value):
+        up_send[k, m] = product(m, 0, value, planes - 1, planes)[:, 0]
+        down_send[k, m] = product(m, 1, value, 0, 1)[:, 0]
+
+    def send(k, m):
+        @pl.when(jnp.logical_not(last))
+        def _():
+            up_copy(k, m).start()
+
+        @pl.when(jnp.logical_not(first))
+        def _():
+            down_copy(k, m).start()
+
+    def inside(m, value):
+        up = product(m, 0, value, 0, planes - 1)
+        down = product(m, 1, value, 1, planes)
+        moved = pltpu.roll(product(m, 2, value, 0, planes), 1, 2)
+        total = jnp.where(col_at == 0, 0.0, moved)
+        moved = pltpu.roll(product(m, 3, value, 0, planes), columns - 1, 2)
+        total = total + jnp.where(col_at == columns - 1, 0.0, moved)
+        moved = pltpu.roll(product(m, 4, value, 0, planes), 1, 3)
+        total = total + jnp.where(lane_at == 0, 0.0, moved)
+        moved = pltpu.roll(product(m, 5, value, 0, planes), layers - 1, 3)
+        total = total + jnp.where(lane_at == layers - 1, 0.0, moved)
+        return source[m] - total, up, down
+
+    for m in range(members):
+        edges(0, m, now[m])
+    loads[5].wait()
+    ids = lax.broadcasted_iota(jnp.int32, (blocks, layers), 0)
+    for x in range(planes):
+        for y in range(columns):
+            row = x * columns + y
+            hit = jnp.where(bmap[x, y : y + 1, :] == ids, 1.0, 0.0)
+            mask[:, row * layers : (row + 1) * layers] = hit.astype(BF16)
+    pl.semaphore_wait(barrier, devices - 1)
+    for m in range(members):
+        send(0, m)
     for k in range(ITERS):
-        for m in range(members):
-            up_send[k, m] = product(m, 0, now[m], planes - 1, planes)[:, 0]
-            down_send[k, m] = product(m, 1, now[m], 0, 1)[:, 0]
-
-            @pl.when(jnp.logical_not(last))
-            def _(m=m):
-                up_copy(k, m).start()
-
-            @pl.when(jnp.logical_not(first))
-            def _(m=m):
-                down_copy(k, m).start()
-
-        inner = []
-        for m in range(members):
-            up = product(m, 0, now[m], 0, planes - 1)
-            down = product(m, 1, now[m], 1, planes)
-            left = pltpu.roll(product(m, 2, now[m], 0, planes), 1, 2)
-            total = jnp.where(col_at == 0, 0.0, left)
-            left = pltpu.roll(product(m, 3, now[m], 0, planes), columns - 1, 2)
-            total = total + jnp.where(col_at == columns - 1, 0.0, left)
-            left = pltpu.roll(product(m, 4, now[m], 0, planes), 1, 3)
-            total = total + jnp.where(lane_at == 0, 0.0, left)
-            left = pltpu.roll(product(m, 5, now[m], 0, planes), layers - 1, 3)
-            total = total + jnp.where(lane_at == layers - 1, 0.0, left)
-            inner.append((source[m] - total, up, down))
-        if k == 0:
-            ids = lax.broadcasted_iota(jnp.int32, (blocks, layers), 0)
-            for x in range(planes):
-                for y in range(columns):
-                    row = x * columns + y
-                    hit = jnp.where(bmap[x, y : y + 1, :] == ids, 1.0, 0.0)
-                    mask[:, row * layers : (row + 1) * layers] = hit.astype(BF16)
+        inner = [inside(m, now[m]) for m in range(members)]
         after = []
         for m in range(members):
             rest, up, down = inner[m]
@@ -198,13 +203,14 @@
 
             rest = rest - jnp.concatenate([below[k, m][:, None], up], axis=1)
             rest = rest - jnp.concatenate([down, above[k, m][:, None]], axis=1)
-            after.append(inverse(m, rest))
+            value = inverse(m, rest)
+            if k < ITERS - 1:
+                edges(k + 1, m, value)
+                send(k + 1, m)
+            else:
+                adj[m] = value
+            after.append(value)
         now = after
-
-    for m in range(members):
-        adj[m] = now[m]
-    save = pltpu.make_async_copy(adj, adj_hbm, adj_sem)
-    save.start()
 
     def gather(i, total):
         pltpu.make_async_copy(sens_hbm.at[i], sens.at[i], sens_sem.at[i]).wait()
@@ -242,7 +248,7 @@
         device_id=next_id, device_id_type=MESH,
     )
     everything.wait_recv()
-    grad_ref[...] = part[me_c] + jnp.sum(got[...], axis=0)
+    got_out[...] = part[me_c] + jnp.sum(got[...], axis=0)
 
     everything.wait_send()
     for k in range(ITERS):
@@ -255,7 +261,16 @@
             def _(k=k, m=m):
                 down_copy(k, m).wait_send()
 
-    save.wait()
+
+def write_out(adjoint, gradient, adjoint_hbm, gradient_hbm, sem):
+    copies = [
+        pltpu.make_async_copy(adjoint, adjoint_hbm, sem.at[0]),
+        pltpu.make_async_copy(gradient, gradient_hbm, sem.at[1]),
+    ]
+    for copy in copies:
+        copy.start()
+    for copy in copies:
+        copy.wait()
 
 
 def solution(mesh):
@@ -272,15 +287,16 @@
         wells = well_cells.reshape(1, -1)
         halo = (ITERS, members, unknowns, columns, layers)
         any_spec = pl.BlockSpec(memory_space=pl.ANY)
+        vmem_spec = pl.BlockSpec(memory_space=pltpu.VMEM)
         dma = pltpu.SemaphoreType.DMA
-        return pl.pallas_call(
+        adjoint, gradient = pl.pallas_call(
             functools.partial(kernel, ranks, groups, blocks),
             out_shape=(
-                jax.ShapeDtypeStruct(later_adjoint.shape, F32),
-                jax.ShapeDtypeStruct((blk_dev, params), F32),
+                pltpu.VMEM(later_adjoint.shape, F32),
+                pltpu.VMEM((blk_dev, params), F32),
             ),
             in_specs=[any_spec] * 7,
-            out_specs=(any_spec, pl.BlockSpec(memory_space=pltpu.VMEM)),
+            out_specs=(vmem_spec, vmem_spec),
             scratch_shapes=[
                 pltpu.VMEM(later_adjoint.shape, F32),
                 pltpu.VMEM(coupling.shape, BF16),
@@ -289,7 +305,6 @@
                 pltpu.VMEM(wells.shape, jnp.int32),
                 pltpu.VMEM(well_misfit.shape, F32),
                 pltpu.VMEM(block_map.shape, jnp.int32),
-                pltpu.VMEM(later_adjoint.shape, F32),
                 pltpu.VMEM(later_adjoint.shape, F32),
                 pltpu.VMEM(halo, F32),
                 pltpu.VMEM(halo, F32),
@@ -301,7 +316,6 @@
                 pltpu.VMEM((ranks * groups - 1, blk_dev, params), F32),
                 dma((6,)),
                 dma((fields,)),
-                dma,
                 dma((ITERS, members)),
                 dma((ITERS, members)),
                 dma((ITERS, members)),
@@ -311,6 +325,16 @@
             ],
             compiler_params=pltpu.CompilerParams(collective_id=0, has_side_effects=True),
         )(later_adjoint, coupling, diag_inverse, sens, wells, well_misfit, block_map)
+        return pl.pallas_call(
+            write_out,
+            out_shape=(
+                jax.ShapeDtypeStruct(adjoint.shape, F32),
+                jax.ShapeDtypeStruct(gradient.shape, F32),
+            ),
+            in_specs=[vmem_spec] * 2,
+            out_specs=(any_spec, any_spec),
+            scratch_shapes=[dma((2,))],
+        )(*[pltpu.with_memory_space_constraint(a, pltpu.VMEM) for a in (adjoint, gradient)])
 
     placed = (
         P("ens", None, "cells", None, None),

time: 28.8 us -> 25.6 us (0.89)
  local copies, waits for them, and re-layouts: 2.72 us -> 0 us
  Pallas kernels: 25.2 us -> 24.8 us
    unnamed x2 -> x0, local copies, waits for them, and re-layouts: 2.72 us -> none
    pallas_call x1, Pallas kernels: 25.2 us -> 24.2 us  [body(): pl.pallas_call(functools.partial(kernel, ranks, groups, blocks), out_shap...]
    pallas_call x0 -> x1, Pallas kernels: none -> 0.65 us  [body(): pl.pallas_call(write_out, out_shape=(jax.ShapeDtypeStruct(adjoint.shape,...]
where the time goes in v2:
time: 25.6 us; the launch traced here: 25.5 us
  Pallas kernels  24.8 us (97%)
  between operations  0.64 us (2%)
    pallas_call x1, Pallas kernels, body(): pl.pallas_call(functools.partial(kernel, ranks, groups, blocks), out_shap...  24.2 us
    pallas_call x1, Pallas kernels, body(): pl.pallas_call(write_out, out_shape=(jax.ShapeDtypeStruct(adjoint.shape,...  0.65 us

profile of v2, /device:TPU:0, one launch (start us, length us, event | category | flops | bytes accessed | tf_op | source)
XLA Modules:
  0.0 25.5 jit_solution(18305844016652150719)
XLA Ops:
  0.6 24.2 %shard_map.86 = (f32[2,4,2,8,128]{4,3,2,1,0:T(8,128)S(1)}, f32[4,128]{1,0:T(4,128)S(1)}) custom-call(f32[2,4,2,8,128]{4,3,2,1,0:T(8,128)} %later_hbm.1, bf16[2,6,4,4,2,8,128]{6,5,4,3,2,1,0:T(8,128)(2,1)} %coup_hbm.1, bf16[2,4,4,2,8,128]{5,4,3,2,1,0:T(8,128)(2,1)} %diag_hbm.1, bf16[8,16,128,128]{3,2,1,0:T(8,128)(2,1)} %bitcast.2, s32[1,256]{1,0:T(1,128)} %bitcast.3, ...), custom_call_target="tpu_custom_call" | custom-call | tf_op jit(solution)/shard_map/pallas_call | solution.py:292
  24.8 0.7 %shard_map.87 = (f32[2,4,2,8,128]{4,3,2,1,0:T(8,128)}, f32[4,128]{1,0:T(4,128)}) custom-call(f32[2,4,2,8,128]{4,3,2,1,0:T(8,128)S(1)} %get-tuple-element.4.adjoint, f32[4,128]{1,0:T(4,128)S(1)} %get-tuple-element.5.gradient), custom_call_target="tpu_custom_call" | custom-call | tf_op jit(solution)/shard_map/pallas_call | solution.py:328

commit v3 on v2

--- a/solution.py
+++ b/solution.py
@@ -36,7 +36,7 @@
     adj, got_out,
     later, coup, diag, sens, wells, misfit, bmap, source,
     up_send, down_send, below, above, mask, lhs, part, got,
-    load_sem, sens_sem, up_ssem, up_rsem, down_ssem, down_rsem, part_ssem, part_rsem,
+    load_sem, sens_sem, up_ssem, up_rsem, down_ssem, down_rsem, part_ssem, part_rsem, here_sem,
 ):
     members, unknowns, planes, columns, layers = later.shape
     rows = planes * columns
@@ -54,10 +54,36 @@
 
     barrier = pltpu.get_barrier_semaphore()
 
-    def greet(step):
-        c, e = other(step)
-        pl.semaphore_signal(barrier, inc=1, device_id=(c, e), device_id_type=MESH)
-
+    bits = devices.bit_length() - 1
+
+    def partner(bit):
+        size = 1 << bit
+        at = me + size - 2 * size * ((me // size) % 2)
+        return at // groups, at % groups
+
+    beside = me_c + 2 * (me_c % 2) - 1
+    has_beside = (beside >= 0) & (beside < ranks)
+
+    def greet_all():
+        @pl.when(has_beside)
+        def _():
+            pl.semaphore_signal(barrier, inc=1, device_id=(beside, me_e), device_id_type=MESH)
+
+        for bit in range(bits):
+            pl.semaphore_signal(barrier, inc=1, device_id=partner(bit), device_id_type=MESH)
+
+    def greeted():
+        pl.semaphore_wait(barrier, jnp.where(has_beside, bits + 1, bits))
+
+    def tell(bit):
+        if bit < bits:
+            pl.semaphore_signal(here_sem.at[bit], inc=1, device_id=partner(bit), device_id_type=MESH)
+
+    def hear(bit):
+        if bit < bits:
+            pl.semaphore_wait(here_sem.at[bit], 1)
+
+    greet_all()
     loads = [
         pltpu.make_async_copy(src, dst, load_sem.at[i])
         for i, (src, dst) in enumerate(
@@ -73,9 +99,6 @@
     sens_loads = [
         pltpu.make_async_copy(sens_hbm.at[i], sens.at[i], sens_sem.at[i]) for i in range(fields)
     ]
-    for load in sens_loads:
-        load.start()
-    for_each(devices - 1, greet)
 
     loads[0].wait()
     loads[1].wait()
@@ -113,6 +136,8 @@
     loads[3].wait()
     now = [inverse(m, source[m]) for m in range(members)]
     loads[4].wait()
+    for load in sens_loads:
+        load.start()
 
     first = me_c == 0
     last = me_c == ranks - 1
@@ -177,18 +202,20 @@
 
     for m in range(members):
         edges(0, m, now[m])
-    loads[5].wait()
-    ids = lax.broadcasted_iota(jnp.int32, (blocks, layers), 0)
-    for x in range(planes):
-        for y in range(columns):
-            row = x * columns + y
-            hit = jnp.where(bmap[x, y : y + 1, :] == ids, 1.0, 0.0)
-            mask[:, row * layers : (row + 1) * layers] = hit.astype(BF16)
-    pl.semaphore_wait(barrier, devices - 1)
+    greeted()
     for m in range(members):
         send(0, m)
+    tell(0)
     for k in range(ITERS):
         inner = [inside(m, now[m]) for m in range(members)]
+        if k == 0:
+            loads[5].wait()
+            ids = lax.broadcasted_iota(jnp.int32, (blocks, layers), 0)
+            for x in range(planes):
+                for y in range(columns):
+                    row = x * columns + y
+                    hit = jnp.where(bmap[x, y : y + 1, :] == ids, 1.0, 0.0)
+                    mask[:, row * layers : (row + 1) * layers] = hit.astype(BF16)
         after = []
         for m in range(members):
             rest, up, down = inner[m]
@@ -211,6 +238,8 @@
                 adj[m] = value
             after.append(value)
         now = after
+        hear(k)
+        tell(k + 1)
 
     def gather(i, total):
         pltpu.make_async_copy(sens_hbm.at[i], sens.at[i], sens_sem.at[i]).wait()
@@ -242,6 +271,10 @@
             device_id=(c, e), device_id_type=MESH,
         )
 
+    hear(ITERS)
+    for bit in range(ITERS + 1, bits):
+        tell(bit)
+        hear(bit)
     for_each(devices - 1, lambda step: part_copy(step).start())
     everything = pltpu.make_async_remote_copy(
         src_ref=got, dst_ref=got, send_sem=part_ssem, recv_sem=part_rsem,
@@ -275,6 +308,7 @@
 
 def solution(mesh):
     ranks, groups = mesh.shape["cells"], mesh.shape["ens"]
+    assert (ranks * groups) & (ranks * groups - 1) == 0
 
     def body(later_adjoint, coupling, diag_inverse, sensitivity, well_cells, well_misfit, block_map):
         members, unknowns, planes, columns, layers = later_adjoint.shape
@@ -322,6 +356,7 @@
                 dma((ITERS, members)),
                 dma,
                 dma,
+                pltpu.SemaphoreType.REGULAR(((ranks * groups).bit_length() - 1,)),
             ],
             compiler_params=pltpu.CompilerParams(collective_id=0, has_side_effects=True),
         )(later_adjoint, coupling, diag_inverse, sens, wells, well_misfit, block_map)

time: 25.6 us -> 25 us (0.977)
  Pallas kernels: 24.8 us -> 24.2 us
    pallas_call x1, Pallas kernels: 24.2 us -> 23.6 us  [body(): pl.pallas_call(functools.partial(kernel, ranks, groups, blocks), out_shap...]
where the time goes in v3:
time: 25 us; the launch traced here: 24.9 us
  Pallas kernels  24.2 us (97%)
  between operations  0.64 us (3%)
    pallas_call x1, Pallas kernels, body(): pl.pallas_call(functools.partial(kernel, ranks, groups, blocks), out_shap...  23.6 us
    pallas_call x1, Pallas kernels, body(): pl.pallas_call(write_out, out_shape=(jax.ShapeDtypeStruct(adjoint.shape,...  0.65 us

profile of v3, /device:TPU:0, one launch (start us, length us, event | category | flops | bytes accessed | tf_op | source)
XLA Modules:
  0.0 24.9 jit_solution(8079713817004415141)
XLA Ops:
  0.6 23.6 %shard_map.86 = (f32[2,4,2,8,128]{4,3,2,1,0:T(8,128)S(1)}, f32[4,128]{1,0:T(4,128)S(1)}) custom-call(f32[2,4,2,8,128]{4,3,2,1,0:T(8,128)} %later_hbm.1, bf16[2,6,4,4,2,8,128]{6,5,4,3,2,1,0:T(8,128)(2,1)} %coup_hbm.1, bf16[2,4,4,2,8,128]{5,4,3,2,1,0:T(8,128)(2,1)} %diag_hbm.1, bf16[8,16,128,128]{3,2,1,0:T(8,128)(2,1)} %bitcast.2, s32[1,256]{1,0:T(1,128)} %bitcast.3, ...), custom_call_target="tpu_custom_call" | custom-call | tf_op jit(solution)/shard_map/pallas_call | solution.py:326
  24.2 0.7 %shard_map.87 = (f32[2,4,2,8,128]{4,3,2,1,0:T(8,128)}, f32[4,128]{1,0:T(4,128)}) custom-call(f32[2,4,2,8,128]{4,3,2,1,0:T(8,128)S(1)} %get-tuple-element.4.adjoint, f32[4,128]{1,0:T(4,128)S(1)} %get-tuple-element.5.gradient), custom_call_target="tpu_custom_call" | custom-call | tf_op jit(solution)/shard_map/pallas_call | solution.py:363
